TPU v7x, 256 devices: a whole 4x4x8 slice. The times are simulated.
256 devices in a mesh: seq: 128 (over y, x_lo, z, core), dp: 2 (over x_hi).
Axes of the slice: x: 4 (x_hi: 2, x_lo: 2; x = x_hi * 2 + x_lo), y: 4, z: 8, core: 2. Of those that a mesh axis runs over, the one named last changes fastest.
Arguments:
- q_student: bfloat16 [2, 65536, 1536], P('dp', 'seq'), may hold values from -8 to 8
- kv_student: bfloat16 [2, 1024, 3072], P('dp', 'seq'), may hold values from -8 to 8
- q_target: bfloat16 [2, 65536, 1536], P('dp', 'seq'), may hold values from -8 to 8
- kv_target: bfloat16 [2, 1024, 3072], P('dp', 'seq'), may hold values from -8 to 8
Outputs:
- student_out: bfloat16 [2, 65536, 1536], P('dp', 'seq')
- target_out: bfloat16 [2, 65536, 1536], P('dp', 'seq')
- distill_loss: float32 [], replicated
All inputs are finite; a program needn't handle non-finite values.
Results may differ from a plain program's by a relative error of at most 0.004.
Values may be sent and summed in bfloat16 or wider, within the bound.
A program may use at most 128 MiB of HBM per device.

v0:
```python
import jax
import jax.numpy as jnp
from jax import lax
from jax.sharding import Mesh
from jax.sharding import PartitionSpec as P

HEADS = 12
HD = 128
SEQ = ("seq_0", "seq_1", "seq_2", "seq_3")
SEQ_DP = ("seq_0", "seq_1", "seq_2", "seq_3", "dp")


def in_one_piece(arrays, axis, dim, along):
    both = jnp.concatenate(arrays, axis=along)
    out, at, finished = (lax.all_gather(both, axis, axis=dim, tiled=True), 0, [])
    for a in arrays:
        finished.append(lax.slice_in_dim(out, at, at + a.shape[along], axis=along))
        at += a.shape[along]
    return tuple(finished)


def over_axes(shard, axes):
    for axis in axes:
        shard = lax.psum(shard, axis)
    return shard


def absorb(query3, carried, incoming):
    running_max, running_sum, running_out = carried
    block_pairs = incoming[0]
    key_rows = block_pairs.shape[0]
    feature_width = HEADS * HD
    key_block = block_pairs[:, :feature_width].reshape(key_rows, HEADS, HD)
    value_block = block_pairs[:, feature_width:].reshape(key_rows, HEADS, HD)
    scores = jnp.einsum("qhd,khd->hqk", query3, key_block, preferred_element_type=jnp.float32) * (
        1.0 / HD**0.5
    )
    new_max = jnp.maximum(running_max, jnp.max(scores, axis=-1))
    exponent = jnp.exp(scores - new_max[:, :, None])
    running_sum = jnp.sum(exponent, axis=-1)
    running_out = jnp.einsum(
        "hqk,khd->hqd",
        exponent.astype(jnp.bfloat16),
        value_block,
        preferred_element_type=jnp.float32,
    )
    return (new_max, running_sum, running_out)


def normalize(carried, query_rows):
    running_max, running_sum, running_out = carried
    mixed_rows = running_out / running_sum[:, :, None]
    return jnp.transpose(mixed_rows, (1, 0, 2)).reshape(query_rows, HEADS * HD)


def body(q_student, kv_student, q_target, kv_target):
    query_rows = q_student.shape[1]
    student_query = q_student[0].reshape(query_rows, HEADS, HD)
    target_query = q_target[0].reshape(query_rows, HEADS, HD)
    initial = (
        jnp.full((HEADS, query_rows), -1e30, jnp.float32),
        jnp.zeros((HEADS, query_rows), jnp.float32),
        jnp.zeros((HEADS, query_rows, HD), jnp.float32),
    )
    incoming = in_one_piece((kv_student, kv_target), SEQ, 1, 0)
    student_carry = absorb(student_query, initial, incoming[0])
    target_carry = absorb(target_query, initial, incoming[1])
    student_rows = normalize(student_carry, query_rows)
    target_rows = normalize(target_carry, query_rows)
    seq_count = lax.axis_size(SEQ)
    all_tokens = query_rows * seq_count
    position = (lax.axis_index(SEQ) * query_rows + jnp.arange(query_rows)).astype(jnp.float32)
    weight = 1.0 + 2.0 * position / float(max(all_tokens - 1, 1))
    gap_rows = student_rows - target_rows
    local_term = jnp.sum(weight[:, None] * gap_rows * gap_rows) / float(all_tokens * HEADS * HD)
    distill_loss = over_axes(local_term, SEQ_DP)
    return (
        student_rows[None].astype(jnp.bfloat16),
        target_rows[None].astype(jnp.bfloat16),
        distill_loss,
    )


def solution(mesh):
    finer = Mesh(
        mesh.devices.reshape(4, 2, 8, 2, mesh.shape["dp"]),
        ("seq_0", "seq_1", "seq_2", "seq_3", "dp"),
    )
    in_specs = (P("dp", SEQ, None), P("dp", SEQ, None), P("dp", SEQ, None), P("dp", SEQ, None))
    out_specs = (P("dp", SEQ, None), P("dp", SEQ, None), P())
    return jax.shard_map(body, mesh=finer, in_specs=in_specs, out_specs=out_specs, check_vma=False)
```

profile of v0, /device:TPU:1, one launch (start us, length us, event | category | flops | bytes accessed | tf_op | source)
XLA Modules:
  0.0 443.3 jit_solution(12665240037221785028)
XLA Ops:
  7.2 0.0 all-gather.2.cloned.1.call-start
  7.2 0.8 pad_maximum_fusion
  8.0 0.7 copy.27
  8.8 0.0 all-gather.2.cloned.1.call-update
  8.8 1.7 copy.34
  10.6 1.7 copy.29
  12.3 226.2 %all-gather.2.cloned.1.call-done = bf16[2,1024,3072]{2,0,1:T(2,128)(2,1)} async-done(((bf16[2,8,3072]{2,0,1:T(2,128)(2,1)}), bf16[2,1024,3072]{2,0,1:T(2,128)(2,1)}) %all-gather.2.cloned.1.call-update) | async-done | bytes 12582928 | tf_op jit(solution)/shard_map/all_gather | solution.py:15
  238.6 24.8 %fusion.21 = (bf16[1,1024,3072]{2,0,1:T(2,128)(2,1)}, bf16[1,1024,3072]{2,0,1:T(2,128)(2,1)}) fusion(bf16[2,1024,3072]{2,0,1:T(2,128)(2,1)} %all-gather.2.cloned.1.call-done), kind=kLoop, calls=%fused_computation.26 | loop fusion | bytes 25165824 | tf_op jit(solution)/shard_map/slice | solution.py:17
  263.3 25.9 %copy.47 = bf16[1,1024,3072]{1,2,0:T(8,128)(2,1)} copy(bf16[1,1024,3072]{2,0,1:T(2,128)(2,1)} %get-tuple-element.12) | data formatting | bytes 12582912
  289.3 5.2 %fusion.22 = (bf16[1024,1536]{0,1:T(8,128)(2,1)S(1)}, bf16[1024,1536]{0,1:T(8,128)(2,1)}) fusion(bf16[1024,3072]{0,1:T(8,128)(2,1)} %bitcast.48), kind=kLoop, calls=%fused_computation.27 | loop fusion | bytes 12582912 | tf_op jit(solution)/shard_map/slice | solution.py:33
  294.5 10.1 %bitcast_reduce_fusion = (f32[12,512]{1,0:T(8,128)S(1)}, f32[12,1024,512]{2,1,0:T(8,128)}) fusion(bf16[1024,12,128]{0,2,1:T(8,128)(2,1)S(1)} %bitcast.50, bf16[512,12,128]{0,2,1:T(8,128)(2,1)S(1)} %bitcast.52), kind=kOutput, calls=%fused_computation.1 | convolution fusion | flops 1623189504 | bytes 29908992 | tf_op jit(solution)/shard_map/qhd,khd->hqk/dot_general | solution.py:35
  304.5 25.9 %copy.46 = bf16[1,1024,3072]{1,2,0:T(8,128)(2,1)} copy(bf16[1,1024,3072]{2,0,1:T(2,128)(2,1)} %get-tuple-element.13) | data formatting | bytes 12582912
  330.5 3.6 fusion.23
  334.0 10.1 %bitcast_reduce_fusion.1 = (f32[12,512]{1,0:T(8,128)S(1)}, f32[12,1024,512]{2,1,0:T(8,128)}) fusion(bf16[1024,12,128]{0,2,1:T(8,128)(2,1)S(1)} %bitcast.51, bf16[512,12,128]{0,2,1:T(8,128)(2,1)S(1)} %bitcast.53), kind=kOutput, calls=%fused_computation.4 | convolution fusion | flops 1623189504 | bytes 29908992 | tf_op jit(solution)/shard_map/qhd,khd->hqk/dot_general | solution.py:35
  344.1 0.0 copy-start
  344.1 10.6 %fusion.4 = f32[12,512]{1,0:T(8,128)S(1)} fusion(f32[12,1024,512]{2,1,0:T(8,128)} %get-tuple-element.24, f32[12,512]{1,0:T(8,128)S(1)} %broadcast_maximum_fusion), kind=kLoop, calls=%fused_computation.8 | loop fusion | flops 18868224 | bytes 25214976 | tf_op jit(solution)/shard_map/reduce_sum | solution.py:40
  354.7 0.0 copy-done
  354.7 12.2 %bitcast_divide_fusion = f32[512,12,128]{0,2,1:T(8,128)} fusion(bf16[1024,12,128]{0,2,1:T(8,128)(2,1)S(1)} %bitcast.54, f32[12,1024,512]{2,1,0:T(8,128)} %get-tuple-element.24, f32[12,512]{1,0:T(8,128)S(1)} %broadcast_maximum_fusion, f32[512,12]{0,1:T(8,128)S(1)} %bitcast.59), kind=kOutput, calls=%fused_computation.18 | convolution fusion | flops 1630273536 | bytes 31506432 | tf_op jit(solution)/shard_map/hqk,khd->hqd/dot_general | solution.py:41
  366.9 10.4 %fusion.2 = f32[12,512]{1,0:T(8,128)S(1)} fusion(f32[12,1024,512]{2,1,0:T(8,128)} %get-tuple-element.22, f32[12,512]{1,0:T(8,128)S(1)} %broadcast_maximum_fusion.1), kind=kLoop, calls=%fused_computation.6 | loop fusion | flops 18868224 | bytes 25214976 | tf_op jit(solution)/shard_map/reduce_sum | solution.py:40
  377.4 13.5 %fusion.14 = (f32[]{:T(128)}, bf16[512,12,128]{0,2,1:T(8,128)(2,1)S(1)}, bf16[512,12,128]{0,2,1:T(8,128)(2,1)S(1)}) fusion(f32[512,12,128]{0,2,1:T(8,128)} %bitcast_divide_fusion, f32[512]{0:T(512)S(1)} %multiply_add_fusion, f32[512,12]{0,1:T(8,128)S(1)} %bitcast.58, bf16[1024,12,128]{0,2,1:T(8,128)(2,1)S(1)} %bitcast.55, ...), kind=kOutput, calls=%fused_computation.17 | convolution fusion | flops 1634992128 | bytes 34654212 | tf_op jit(solution)/shard_map/hqk,khd->hqd/dot_general | solution.py:41
  391.6 6.8 %psum.35 = f32[]{:T(128)} all-reduce(f32[]{:T(128)S(6)} %div.39), channel_id=1, replica_groups=mesh['seq_0'=4,'seq_1'=2,'seq_2'=8,'seq_3'=2,'dp'=2] {'seq_0'}, use_global_device_ids=true, to_apply=%region_5.0 | all-reduce | flops 1 | bytes 8 | tf_op jit(solution)/shard_map/psum | solution.py:24
  398.3 4.4 psum.36
  402.7 13.9 %psum.37 = f32[]{:T(128)} all-reduce(f32[]{:T(128)} %psum.36), channel_id=1, replica_groups=mesh['seq_0'=4,'seq_1'=2,'seq_2'=8,'seq_3'=2,'dp'=2] {'seq_2'}, use_global_device_ids=true, to_apply=%region_7.0 | all-reduce | flops 1 | bytes 8 | tf_op jit(solution)/shard_map/psum | solution.py:24
  416.6 1.6 copy.38
  418.2 10.8 %psum.38 = f32[]{:T(128)} all-reduce(f32[]{:T(128)} %psum.37), channel_id=1, replica_groups=mesh['seq_0'=4,'seq_1'=2,'seq_2'=8,'seq_3'=2,'dp'=2] {'seq_3'}, use_global_device_ids=true, to_apply=%region_8.0 | all-reduce | flops 1 | bytes 8 | tf_op jit(solution)/shard_map/psum | solution.py:24
  429.0 1.6 copy.39
  430.5 5.9 %psum.39 = f32[]{:T(128)} all-reduce(f32[]{:T(128)} %psum.38), channel_id=1, replica_groups=mesh['seq_0'=4,'seq_1'=2,'seq_2'=8,'seq_3'=2,'dp'=2] {'dp'}, use_global_device_ids=true, to_apply=%region_9.0 | all-reduce | flops 1 | bytes 8 | tf_op jit(solution)/shard_map/psum | solution.py:24
  (3 shorter events, 0.0 us)
Async XLA Ops:
  7.2 231.4 %all-gather.2.cloned.1.call-start = ((), (), s32[]{:S(2)}) async-start(), calls=%async_computation | async-start | bytes 12681216 | tf_op jit(solution)/shard_map/all_gather | solution.py:15
  344.1 10.6 %copy-start = (bf16[1024,1536]{0,1:T(8,128)(2,1)S(1)}, bf16[1024,1536]{0,1:T(8,128)(2,1)}, u32[]{:S(2)}) copy-start(bf16[1024,1536]{0,1:T(8,128)(2,1)} %get-tuple-element.15) | copy-start | bytes 9437188
Sparse Core Ops, SparseCore 0:
  10.4 228.0 all-gather.1
where the time goes:
time: 445 us; the launch traced here: 443 us
  waiting for transfers between devices  226 us (51%)
  local copies, waits for them, and re-layouts  92.7 us (21%)
  matrix products  45.9 us (10%)
  blocking collectives  41.7 us (9%)
  other arithmetic  21.9 us (5%)
  between operations  14.8 us (3%)
    all_gather x1, waiting for transfers between devices, in_one_piece(): lax.all_gather(both, axis, axis=dim, tiled=True)  226 us
    unnamed x8, local copies, waits for them, and re-layouts  58.4 us
    psum x5, blocking collectives, over_axes(): shard = lax.psum(shard, axis)  41.7 us
    dot_general x2, matrix products, absorb(): jnp.einsum('hqk,khd->hqd', exponent.astype(jnp.bfloat16), value_block, pr...  25.8 us
    slice x1, local copies, waits for them, and re-layouts, in_one_piece(): finished.append(lax.slice_in_dim(out, at, at + a.shape[along], axis=along))  24.8 us
    reduce_sum x2, other arithmetic, absorb(): running_sum = jnp.sum(exponent, axis=-1)  21 us
    dot_general x2, matrix products, absorb(): jnp.einsum('qhd,khd->hqk', query3, key_block, preferred_element_type=jnp....  20.1 us
  transfers between devices with their start and end apart: 1, of which 1 were waited for; matrix products, arithmetic and copies ran while one was open for 1% of the time, Pallas kernels for 0%

commit v1 on v0

v1 whole, which is shorter than its diff:
```python
import functools
import heapq

import jax
import jax.numpy as jnp
from jax import lax
from jax.experimental import pallas as pl
from jax.experimental.pallas import tpu as pltpu
from jax.sharding import PartitionSpec as P

HEADS = 12
HD = 128
WIDTH = HEADS * HD
NY, NX, NZ = 4, 2, 8
SIZE = {"y": NY, "x": NX, "z": NZ}
AXIS = {"y": 0, "x": 1, "z": 2}
ROWS = 8
SLOTS = 2 * NY * NX * NZ
LINES = NY * NX
LOG2E = 1.4426950408889634
TREES = (("zyx", 0, 1536), ("zxy", 1536, 3840), ("yxz", 3840, 6144))


def signed(axis, v, d, salt):
    n = SIZE[axis]
    if axis == "x":
        return v
    if v * 2 == n:
        return v if (sum(d) - v + salt) % 2 == 0 else -v
    return v if v * 2 < n else v - n


def last_hop(order, d, salt):
    for axis in reversed(order):
        v = d[AXIS[axis]]
        if v:
            return axis, (1 if signed(axis, v, d, salt) > 0 else -1)
    return None


def children(order, d, salt):
    out = []
    for axis in "zyx":
        for s in (1, -1) if axis != "x" else (1,):
            nd = list(d)
            nd[AXIS[axis]] = (nd[AXIS[axis]] + s) % SIZE[axis]
            nd = tuple(nd)
            if nd != (0, 0, 0) and last_hop(order, nd, salt) == (axis, s):
                out.append((axis, s, nd))
    return out


def height(order, d, salt):
    return max([1 + height(order, c[2], salt) for c in children(order, d, salt)] or [0])


def relay_order():
    heap = [(0.0, k, k, (0, 0, 0)) for k in range(len(TREES))]
    count, free, core, order = len(TREES), {}, 0.0, []
    while heap:
        t, _, k, d = heapq.heappop(heap)
        name, lo, hi = TREES[k]
        core = max(core, t)
        kids = sorted(children(name, d, k), key=lambda c: -height(name, c[2], k))
        order.append((k, d, kids))
        for axis, s, nd in kids:
            core += 0.05
            end = max(core, free.get((axis, s), 0.0)) + (hi - lo) * 16 / 46.7e3
            free[(axis, s)] = end
            heapq.heappush(heap, (end + 1.9, count, k, nd))
            count += 1
    return order


def attend(q_ref, buf, col, head, kk, vv, rows):
    cols = pl.ds(pl.multiple_of(col + head * HD, HD), HD)
    vcols = pl.ds(pl.multiple_of(col + WIDTH + head * HD, HD), HD)
    key = buf[:, :, cols].astype(jnp.float32).reshape(SLOTS * ROWS, HD).astype(jnp.bfloat16)
    kk[:, :HD] = key
    kk[:, HD:] = key
    vv[:, :HD] = buf[:, :, vcols].astype(jnp.float32).reshape(SLOTS * ROWS, HD).astype(jnp.bfloat16)
    outs = []
    for r in range(0, q_ref.shape[0], rows):
        q = q_ref[r : r + rows, pl.ds(pl.multiple_of(head * HD, HD), HD)]
        scaled = q.astype(jnp.float32) * (LOG2E / HD**0.5)
        high = scaled.astype(jnp.bfloat16)
        low = (scaled - high.astype(jnp.float32)).astype(jnp.bfloat16)
        both = jnp.concatenate([high, low], axis=1)
        scores = lax.dot_general(both, kk[...], (((1,), (1,)), ((), ())), preferred_element_type=jnp.float32)
        expo = jnp.exp2(scores - jnp.max(scores, axis=1, keepdims=True)).astype(jnp.bfloat16)
        mixed = jnp.dot(expo, vv[...], preferred_element_type=jnp.float32)
        outs.append(mixed[:, :HD] / mixed[:, HD:])
    return outs


def kernel(
    qs_hbm, kvs_hbm, qt_hbm, kvt_hbm, os_hbm, ot_hbm, loss_ref,
    buf, qs, qt, outs, outt, kk, vv, acc,
    load_sem, q_sem, out_sem, ici_send, d2d_send, ici_recv, d2d_recv,
):
    seq = lax.axis_index("seq")
    core = lax.rem(seq, 2)
    z = lax.rem(seq // 2, NZ)
    x = lax.rem(seq // (2 * NZ), NX)
    y = seq // (2 * NZ * NX)

    def device(yy, xx, zz, cc):
        return {"seq": ((yy * NX + xx) * NZ + zz) * 2 + cc}

    def line(cc, yy, xx):
        return ((cc * NY + yy) * NX + xx) * NZ

    near = {
        ("z", 1): device(y, x, lax.rem(z + 1, NZ), core),
        ("z", -1): device(y, x, lax.rem(z + NZ - 1, NZ), core),
        ("y", 1): device(lax.rem(y + 1, NY), x, z, core),
        ("y", -1): device(lax.rem(y + NY - 1, NY), x, z, core),
        ("x", 1): device(y, 1 - x, z, core),
    }
    partner = device(y, x, z, 1 - core)
    ys = [lax.rem(y + NY - d, NY) for d in range(NY)]
    xs = [x, 1 - x]
    zs = [lax.rem(z + NZ - d, NZ) for d in range(NZ)]

    mine = line(core, y, x) + z
    load_s = pltpu.make_async_copy(kvs_hbm.at[0], buf.at[mine, :, : 2 * WIDTH], load_sem.at[0])
    load_t = pltpu.make_async_copy(kvt_hbm.at[0], buf.at[mine, :, 2 * WIDTH :], load_sem.at[1])
    load_s.start()
    load_t.start()
    barrier = pltpu.get_barrier_semaphore()
    for peer in list(near.values()) + [partner]:
        pl.semaphore_signal(barrier, inc=1, device_id=peer, device_id_type=pl.DeviceIdType.MESH)
    load_q = [
        pltpu.make_async_copy(qs_hbm.at[0], qs, q_sem.at[0]),
        pltpu.make_async_copy(qt_hbm.at[0], qt, q_sem.at[1]),
    ]
    for c in load_q:
        c.start()
    vv[:, HD:] = jnp.ones((SLOTS * ROWS, HD), jnp.bfloat16)
    acc[...] = jnp.zeros_like(acc)
    load_s.wait()
    load_t.wait()
    pl.semaphore_wait(barrier, 6)

    def remote(part, send, recv, to):
        return pltpu.make_async_remote_copy(
            src_ref=part, dst_ref=part, send_sem=send, recv_sem=recv,
            device_id=to, device_id_type=pl.DeviceIdType.MESH,
        )

    def item(k, d):
        _, lo, hi = TREES[k]
        return buf.at[line(core, ys[d[0]], xs[d[1]]) + zs[d[2]], :, lo:hi]

    def sem_of(k, d):
        return ici_recv.at[k, (d[0] * NX + d[1]) * NZ + d[2]]

    have = {}
    for k, d, kids in relay_order():
        _, lo, hi = TREES[k]
        if d != (0, 0, 0):
            remote(item(k, d), ici_send.at[k], sem_of(k, d), partner).wait_recv()
        for axis, s, nd in kids:
            remote(item(k, d), ici_send.at[k], sem_of(k, nd), near[(axis, s)]).start()
        spot = (k, d[0], d[1])
        have[spot] = have.get(spot, 0) + 1
        if have[spot] == NZ:
            part = buf.at[pl.ds(line(core, ys[d[0]], xs[d[1]]), NZ), :, lo:hi]
            remote(part, d2d_send.at[k], d2d_recv.at[k], partner).start()
    for k, (_, lo, hi) in enumerate(TREES):
        part = buf.at[pl.ds((1 - core) * LINES * NZ, LINES * NZ), :, lo:hi]
        remote(part, d2d_send.at[k], d2d_recv.at[k], partner).wait_recv()
    for c in load_q:
        c.wait()

    rows = qs.shape[0]
    block = 256

    def one_head(head, carry):
        a = attend(qs, buf, 0, head, kk, vv, block)
        b = attend(qt, buf, 2 * WIDTH, head, kk, vv, block)
        cols = pl.ds(pl.multiple_of(head * HD, HD), HD)
        for i, (s, t) in enumerate(zip(a, b)):
            at = pl.ds(i * block, block)
            outs[at, cols] = s.astype(jnp.bfloat16)
            outt[at, cols] = t.astype(jnp.bfloat16)
            gap = s - t
            acc[at, :] += gap * gap
        pltpu.make_async_copy(outs.at[:, cols], os_hbm.at[0, :, cols], out_sem.at[0]).start()
        pltpu.make_async_copy(outt.at[:, cols], ot_hbm.at[0, :, cols], out_sem.at[1]).start()
        return carry

    lax.fori_loop(0, HEADS, one_head, 0)

    spot = lax.broadcasted_iota(jnp.int32, (rows, HD), 0) + ((y * NX + x) * NZ + z) * 2 * rows + core * rows
    weight = 1.0 + 2.0 * spot.astype(jnp.float32) / float(rows * SLOTS - 1)
    loss_ref[...] = jnp.sum((weight * acc[...]).reshape(rows // 8, 8, HD), axis=0)

    for k, (_, lo, hi) in enumerate(TREES):
        part = buf.at[pl.ds(0, LINES * NZ - 1), :, lo:hi]
        remote(part, ici_send.at[k], d2d_recv.at[k], partner).wait_send()
        part = buf.at[pl.ds(0, LINES * NZ), :, lo:hi]
        remote(part, d2d_send.at[k], d2d_recv.at[k], partner).wait_send()
    pltpu.make_async_copy(outs, os_hbm.at[0], out_sem.at[0]).wait()
    pltpu.make_async_copy(outt, ot_hbm.at[0], out_sem.at[1]).wait()


def body(q_student, kv_student, q_target, kv_target):
    rows = q_student.shape[1]
    any_space = pl.BlockSpec(memory_space=pl.ANY)
    out = jax.ShapeDtypeStruct(q_student.shape, jnp.bfloat16)
    bf = jnp.bfloat16
    student, target, part = pl.pallas_call(
        kernel,
        out_shape=(out, out, jax.ShapeDtypeStruct((8, HD), jnp.float32)),
        in_specs=[any_space] * 4,
        out_specs=(any_space, any_space, pl.BlockSpec(memory_space=pltpu.VMEM)),
        scratch_shapes=[
            pltpu.VMEM((SLOTS, ROWS, 4 * WIDTH), bf),
            pltpu.VMEM((rows, WIDTH), bf),
            pltpu.VMEM((rows, WIDTH), bf),
            pltpu.VMEM((rows, WIDTH), bf),
            pltpu.VMEM((rows, WIDTH), bf),
            pltpu.VMEM((SLOTS * ROWS, 2 * HD), bf),
            pltpu.VMEM((SLOTS * ROWS, 2 * HD), bf),
            pltpu.VMEM((rows, HD), jnp.float32),
            pltpu.SemaphoreType.DMA((2,)),
            pltpu.SemaphoreType.DMA((2,)),
            pltpu.SemaphoreType.DMA((2,)),
            pltpu.SemaphoreType.DMA((len(TREES),)),
            pltpu.SemaphoreType.DMA((len(TREES),)),
            pltpu.SemaphoreType.DMA((len(TREES), LINES * NZ)),
            pltpu.SemaphoreType.DMA((len(TREES),)),
        ],
        compiler_params=pltpu.CompilerParams(
            collective_id=0, has_side_effects=True, vmem_limit_bytes=60 * 1024 * 1024
        ),
    )(q_student, kv_student, q_target, kv_target)
    total = jnp.sum(part) / float(2 * rows * SLOTS // 2 * WIDTH)
    return student, target, lax.psum(total, ("seq", "dp"))


def solution(mesh):
    spec = P("dp", "seq", None)
    return jax.shard_map(
        body, mesh=mesh, in_specs=(spec,) * 4, out_specs=(spec, spec, P()), check_vma=False
    )
```

time: 445 us -> 155 us (0.35)
  waiting for transfers between devices: 226 us -> 0 us
  local copies, waits for them, and re-layouts: 92.7 us -> 3.92 us
  Pallas kernels: 0 us -> 72 us
  matrix products: 45.9 us -> 0 us
  blocking collectives: 41.7 us -> 75.9 us
  other arithmetic: 21.9 us -> 1.29 us
  between operations: 14.8 us -> 1.29 us
    all_gather x1 -> x0, waiting for transfers between devices: 226 us -> none  [in_one_piece(): lax.all_gather(both, axis, axis=dim, tiled=True)]
    pallas_call x0 -> x1, Pallas kernels: none -> 72 us  [body(): pl.pallas_call(kernel, out_shape=(out, out, jax.ShapeDtypeStruct((8, HD),...]
    unnamed x8 -> x4, local copies, waits for them, and re-layouts: 58.4 us -> 3.92 us
    dot_general x4 -> x0, matrix products: 45.9 us -> none  [the longest x2 25.8 us: absorb(): jnp.einsum('hqk,khd->hqd', exponent.astype(jnp.bfloat16), value_block, pr...]
    psum x5 -> x1, blocking collectives: 41.7 us -> 75.9 us  [body(): return (student, target, lax.psum(total, ('seq', 'dp')))]
    slice x3 -> x0, local copies, waits for them, and re-layouts: 33.5 us -> none  [the longest x1 24.8 us: in_one_piece(): finished.append(lax.slice_in_dim(out, at, at + a.shape[along], axis=along))]
    reduce_sum x2 -> x1, other arithmetic: 21 us -> 1.29 us  [body(): total = jnp.sum(part) / float(2 * rows * SLOTS // 2 * WIDTH)]
  transfers between devices with their start and end apart: 1 -> 0, of which waited for: 1 -> 0; matrix products, arithmetic and copies ran while one was open for 1% -> 0% of each run, Pallas kernels for 0% -> 0%
where the time goes in v1:
time: 155 us; the launch traced here: 154 us
  blocking collectives  75.9 us (49%)
  Pallas kernels  72 us (46%)
  local copies, waits for them, and re-layouts  3.92 us (3%)
    psum x1, blocking collectives, body(): return (student, target, lax.psum(total, ('seq', 'dp')))  75.9 us
    pallas_call x1, Pallas kernels, body(): pl.pallas_call(kernel, out_shape=(out, out, jax.ShapeDtypeStruct((8, HD),...  72 us
    unnamed x4, local copies, waits for them, and re-layouts  3.92 us

profile of v1, /device:TPU:1, one launch (start us, length us, event | category | flops | bytes accessed | tf_op | source)
XLA Modules:
  0.0 154.4 jit_solution(14909257985158327369)
XLA Ops:
  0.6 72.0 %shard_map.67 = (bf16[1,512,1536]{2,1,0:T(8,128)(2,1)}, bf16[1,512,1536]{2,1,0:T(8,128)(2,1)}, f32[8,128]{1,0:T(8,128)}) custom-call(bf16[1,512,1536]{2,1,0:T(8,128)(2,1)} %qs_hbm.1, bf16[1,8,3072]{2,1,0:T(8,128)(2,1)} %kvs_hbm.1, bf16[1,512,1536]{2,1,0:T(8,128)(2,1)} %qt_hbm.1, bf16[1,8,3072]{2,1,0:T(8,128)(2,1)} %kvt_hbm.1), custom_call_target="tpu_custom_call" | custom-call | tf_op jit(solution)/shard_map/pallas_call | solution.py:213
  72.6 1.3 reduce_sum.9
  74.6 75.9 %psum.7 = f32[]{:T(128)} all-reduce(f32[]{:T(128)S(6)} %div.3), channel_id=1, replica_groups=mesh['seq'=128,'dp'=2] {'seq','dp'}, use_global_device_ids=true, to_apply=%region_1.0 | all-reduce | flops 1 | bytes 8 | tf_op jit(solution)/shard_map/psum | solution.py:240
  150.4 0.0 copy-start
  150.4 2.8 %copy.9 = bf16[1,512,1536]{2,1,0:T(8,128)(2,1)} copy(bf16[1,512,1536]{2,1,0:T(8,128)(2,1)} %get-tuple-element.12) | data formatting | bytes 3145728
  153.2 0.0 copy-done
  153.2 1.1 copy.10
Async XLA Ops:
  150.4 2.8 %copy-start = (bf16[1,512,1536]{2,1,0:T(8,128)(2,1)S(1)}, bf16[1,512,1536]{2,1,0:T(8,128)(2,1)}, u32[]{:S(2)}) copy-start(bf16[1,512,1536]{2,1,0:T(8,128)(2,1)} %get-tuple-element.13) | copy-start | bytes 4718596

commit v2 on v1

--- a/solution.py
+++ b/solution.py
@@ -17,6 +17,7 @@
 ROWS = 8
 SLOTS = 2 * NY * NX * NZ
 LINES = NY * NX
+UNROLL = 4
 LOG2E = 1.4426950408889634
 TREES = (("zyx", 0, 1536), ("zxy", 1536, 3840), ("yxz", 3840, 6144))
 
@@ -75,19 +76,14 @@
 def attend(q_ref, buf, col, head, kk, vv, rows):
     cols = pl.ds(pl.multiple_of(col + head * HD, HD), HD)
     vcols = pl.ds(pl.multiple_of(col + WIDTH + head * HD, HD), HD)
-    key = buf[:, :, cols].astype(jnp.float32).reshape(SLOTS * ROWS, HD).astype(jnp.bfloat16)
-    kk[:, :HD] = key
-    kk[:, HD:] = key
+    kk[...] = buf[:, :, cols].astype(jnp.float32).reshape(SLOTS * ROWS, HD).astype(jnp.bfloat16)
     vv[:, :HD] = buf[:, :, vcols].astype(jnp.float32).reshape(SLOTS * ROWS, HD).astype(jnp.bfloat16)
     outs = []
     for r in range(0, q_ref.shape[0], rows):
         q = q_ref[r : r + rows, pl.ds(pl.multiple_of(head * HD, HD), HD)]
-        scaled = q.astype(jnp.float32) * (LOG2E / HD**0.5)
-        high = scaled.astype(jnp.bfloat16)
-        low = (scaled - high.astype(jnp.float32)).astype(jnp.bfloat16)
-        both = jnp.concatenate([high, low], axis=1)
-        scores = lax.dot_general(both, kk[...], (((1,), (1,)), ((), ())), preferred_element_type=jnp.float32)
-        expo = jnp.exp2(scores - jnp.max(scores, axis=1, keepdims=True)).astype(jnp.bfloat16)
+        scores = lax.dot_general(q, kk[...], (((1,), (1,)), ((), ())), preferred_element_type=jnp.float32)
+        scores = (scores - jnp.max(scores, axis=1, keepdims=True)) * (LOG2E / HD**0.5)
+        expo = jnp.exp2(scores).astype(jnp.bfloat16)
         mixed = jnp.dot(expo, vv[...], preferred_element_type=jnp.float32)
         outs.append(mixed[:, :HD] / mixed[:, HD:])
     return outs
@@ -96,16 +92,17 @@
 def kernel(
     qs_hbm, kvs_hbm, qt_hbm, kvt_hbm, os_hbm, ot_hbm, loss_ref,
     buf, qs, qt, outs, outt, kk, vv, acc,
-    load_sem, q_sem, out_sem, ici_send, d2d_send, ici_recv, d2d_recv,
+    total_in, total_out, load_sem, q_sem, out_sem, ici_send, d2d_send, ici_recv, d2d_recv, sum_send, sum_recv,
 ):
     seq = lax.axis_index("seq")
+    dp = lax.axis_index("dp")
     core = lax.rem(seq, 2)
     z = lax.rem(seq // 2, NZ)
     x = lax.rem(seq // (2 * NZ), NX)
     y = seq // (2 * NZ * NX)
 
-    def device(yy, xx, zz, cc):
-        return {"seq": ((yy * NX + xx) * NZ + zz) * 2 + cc}
+    def device(yy, xx, zz, cc, dd=dp):
+        return {"seq": ((yy * NX + xx) * NZ + zz) * 2 + cc, "dp": dd}
 
     def line(cc, yy, xx):
         return ((cc * NY + yy) * NX + xx) * NZ
@@ -122,13 +119,23 @@
     xs = [x, 1 - x]
     zs = [lax.rem(z + NZ - d, NZ) for d in range(NZ)]
 
+    cube = []
+    for i in range(1, 8):
+        cube.append(device(y, lax.rem(x + i // 4, 2), z, lax.rem(core + i // 2 % 2, 2), lax.rem(dp + i % 2, 2)))
+    sums = (
+        ((x * 2 + core) * 2 + dp, cube),
+        (y, [device(lax.rem(y + i, NY), x, z, core) for i in range(1, NY)]),
+        (z, [device(y, x, lax.rem(z + i, NZ), core) for i in range(1, NZ)]),
+    )
+    peers = [p for _, group in sums for p in group]
+
     mine = line(core, y, x) + z
     load_s = pltpu.make_async_copy(kvs_hbm.at[0], buf.at[mine, :, : 2 * WIDTH], load_sem.at[0])
     load_t = pltpu.make_async_copy(kvt_hbm.at[0], buf.at[mine, :, 2 * WIDTH :], load_sem.at[1])
     load_s.start()
     load_t.start()
     barrier = pltpu.get_barrier_semaphore()
-    for peer in list(near.values()) + [partner]:
+    for peer in peers:
         pl.semaphore_signal(barrier, inc=1, device_id=peer, device_id_type=pl.DeviceIdType.MESH)
     load_q = [
         pltpu.make_async_copy(qs_hbm.at[0], qs, q_sem.at[0]),
@@ -136,11 +143,11 @@
     ]
     for c in load_q:
         c.start()
-    vv[:, HD:] = jnp.ones((SLOTS * ROWS, HD), jnp.bfloat16)
+    vv[:, :, :, HD:] = jnp.ones((UNROLL, 2, SLOTS * ROWS, HD), jnp.bfloat16)
     acc[...] = jnp.zeros_like(acc)
     load_s.wait()
     load_t.wait()
-    pl.semaphore_wait(barrier, 6)
+    pl.semaphore_wait(barrier, len(peers))
 
     def remote(part, send, recv, to):
         return pltpu.make_async_remote_copy(
@@ -176,25 +183,40 @@
     rows = qs.shape[0]
     block = 256
 
-    def one_head(head, carry):
-        a = attend(qs, buf, 0, head, kk, vv, block)
-        b = attend(qt, buf, 2 * WIDTH, head, kk, vv, block)
-        cols = pl.ds(pl.multiple_of(head * HD, HD), HD)
-        for i, (s, t) in enumerate(zip(a, b)):
-            at = pl.ds(i * block, block)
-            outs[at, cols] = s.astype(jnp.bfloat16)
-            outt[at, cols] = t.astype(jnp.bfloat16)
-            gap = s - t
-            acc[at, :] += gap * gap
+    def some_heads(step, carry):
+        for u in range(UNROLL):
+            head = step * UNROLL + u
+            a = attend(qs, buf, 0, head, kk.at[u, 0], vv.at[u, 0], block)
+            b = attend(qt, buf, 2 * WIDTH, head, kk.at[u, 1], vv.at[u, 1], block)
+            cols = pl.ds(pl.multiple_of(head * HD, HD), HD)
+            for i, (s, t) in enumerate(zip(a, b)):
+                at = pl.ds(i * block, block)
+                outs[at, cols] = s.astype(jnp.bfloat16)
+                outt[at, cols] = t.astype(jnp.bfloat16)
+                gap = s - t
+                acc[at, :] += gap * gap
+        cols = pl.ds(pl.multiple_of(step * (UNROLL * HD), HD), UNROLL * HD)
         pltpu.make_async_copy(outs.at[:, cols], os_hbm.at[0, :, cols], out_sem.at[0]).start()
         pltpu.make_async_copy(outt.at[:, cols], ot_hbm.at[0, :, cols], out_sem.at[1]).start()
         return carry
 
-    lax.fori_loop(0, HEADS, one_head, 0)
+    lax.fori_loop(0, HEADS // UNROLL, some_heads, 0)
 
     spot = lax.broadcasted_iota(jnp.int32, (rows, HD), 0) + ((y * NX + x) * NZ + z) * 2 * rows + core * rows
     weight = 1.0 + 2.0 * spot.astype(jnp.float32) / float(rows * SLOTS - 1)
-    loss_ref[...] = jnp.sum((weight * acc[...]).reshape(rows // 8, 8, HD), axis=0)
+    total = jnp.sum((weight * acc[...]).reshape(rows // 8, 8, HD), axis=0)
+    for i, (spot, group) in enumerate(sums):
+        total_out[i] = total
+        total_in[i, spot] = total
+        for to in group:
+            pltpu.make_async_remote_copy(
+                src_ref=total_out.at[i], dst_ref=total_in.at[i, spot], send_sem=sum_send.at[i],
+                recv_sem=sum_recv.at[i], device_id=to, device_id_type=pl.DeviceIdType.MESH,
+            ).start()
+        every = total_in.at[i, pl.ds(0, len(group))]
+        remote(every, sum_send.at[i], sum_recv.at[i], partner).wait()
+        total = jnp.sum(total_in[i, : len(group) + 1], axis=0)
+    loss_ref[0, 0] = jnp.sum(total) / float(rows * SLOTS * WIDTH)
 
     for k, (_, lo, hi) in enumerate(TREES):
         part = buf.at[pl.ds(0, LINES * NZ - 1), :, lo:hi]
@@ -212,18 +234,20 @@
     bf = jnp.bfloat16
     student, target, part = pl.pallas_call(
         kernel,
-        out_shape=(out, out, jax.ShapeDtypeStruct((8, HD), jnp.float32)),
+        out_shape=(out, out, jax.ShapeDtypeStruct((1, 1), jnp.float32)),
         in_specs=[any_space] * 4,
-        out_specs=(any_space, any_space, pl.BlockSpec(memory_space=pltpu.VMEM)),
+        out_specs=(any_space, any_space, pl.BlockSpec(memory_space=pltpu.SMEM)),
         scratch_shapes=[
             pltpu.VMEM((SLOTS, ROWS, 4 * WIDTH), bf),
             pltpu.VMEM((rows, WIDTH), bf),
             pltpu.VMEM((rows, WIDTH), bf),
             pltpu.VMEM((rows, WIDTH), bf),
             pltpu.VMEM((rows, WIDTH), bf),
-            pltpu.VMEM((SLOTS * ROWS, 2 * HD), bf),
-            pltpu.VMEM((SLOTS * ROWS, 2 * HD), bf),
+            pltpu.VMEM((UNROLL, 2, SLOTS * ROWS, HD), bf),
+            pltpu.VMEM((UNROLL, 2, SLOTS * ROWS, 2 * HD), bf),
             pltpu.VMEM((rows, HD), jnp.float32),
+            pltpu.VMEM((3, 8, 8, HD), jnp.float32),
+            pltpu.VMEM((3, 8, HD), jnp.float32),
             pltpu.SemaphoreType.DMA((2,)),
             pltpu.SemaphoreType.DMA((2,)),
             pltpu.SemaphoreType.DMA((2,)),
@@ -231,13 +255,14 @@
             pltpu.SemaphoreType.DMA((len(TREES),)),
             pltpu.SemaphoreType.DMA((len(TREES), LINES * NZ)),
             pltpu.SemaphoreType.DMA((len(TREES),)),
+            pltpu.SemaphoreType.DMA((3,)),
+            pltpu.SemaphoreType.DMA((3,)),
         ],
         compiler_params=pltpu.CompilerParams(
             collective_id=0, has_side_effects=True, vmem_limit_bytes=60 * 1024 * 1024
         ),
     )(q_student, kv_student, q_target, kv_target)
-    total = jnp.sum(part) / float(2 * rows * SLOTS // 2 * WIDTH)
-    return student, target, lax.psum(total, ("seq", "dp"))
+    return student, target, part[0, 0]
 
 
 def solution(mesh):

time: 155 us -> 85.3 us (0.55)
  blocking collectives: 75.9 us -> 0 us
  Pallas kernels: 72 us -> 78.5 us
    psum x1 -> x0, blocking collectives: 75.9 us -> none  [body(): return (student, target, lax.psum(total, ('seq', 'dp')))]
    pallas_call x1, Pallas kernels: 72 us -> 78.5 us  [body(): pl.pallas_call(kernel, out_shape=(out, out, jax.ShapeDtypeStruct((1, 1),...]
where the time goes in v2:
time: 85.3 us; the launch traced here: 84.9 us
  Pallas kernels  78.5 us (92%)
  local copies, waits for them, and re-layouts  3.92 us (5%)
  between operations  2.47 us (3%)
    pallas_call x1, Pallas kernels, body(): pl.pallas_call(kernel, out_shape=(out, out, jax.ShapeDtypeStruct((1, 1),...  78.5 us
    unnamed x4, local copies, waits for them, and re-layouts  3.92 us

profile of v2, /device:TPU:1, one launch (start us, length us, event | category | flops | bytes accessed | tf_op | source)
XLA Modules:
  0.0 84.9 jit_solution(18083193608707722458)
XLA Ops:
  0.6 78.5 %shard_map.67 = (bf16[1,512,1536]{2,1,0:T(8,128)(2,1)}, bf16[1,512,1536]{2,1,0:T(8,128)(2,1)}, f32[1,1]{1,0:T(1,128)}) custom-call(bf16[1,512,1536]{2,1,0:T(8,128)(2,1)} %qs_hbm.1, bf16[1,8,3072]{2,1,0:T(8,128)(2,1)} %kvs_hbm.1, bf16[1,512,1536]{2,1,0:T(8,128)(2,1)} %qt_hbm.1, bf16[1,8,3072]{2,1,0:T(8,128)(2,1)} %kvt_hbm.1), custom_call_target="tpu_custom_call" | custom-call | tf_op jit(solution)/shard_map/pallas_call | solution.py:235
  79.2 0.0 copy-start
  79.2 2.8 %copy.10 = bf16[1,512,1536]{2,1,0:T(8,128)(2,1)} copy(bf16[1,512,1536]{2,1,0:T(8,128)(2,1)} %get-tuple-element.12) | data formatting | bytes 3145728
  82.0 0.0 copy-done
  82.0 1.1 %copy.11 = bf16[1,512,1536]{2,1,0:T(8,128)(2,1)} copy(bf16[1,512,1536]{2,1,0:T(8,128)(2,1)S(1)} %copy-done) | data formatting | bytes 3145728
Async XLA Ops:
  79.2 2.8 %copy-start = (bf16[1,512,1536]{2,1,0:T(8,128)(2,1)S(1)}, bf16[1,512,1536]{2,1,0:T(8,128)(2,1)}, u32[]{:S(2)}) copy-start(bf16[1,512,1536]{2,1,0:T(8,128)(2,1)} %get-tuple-element.13) | copy-start | bytes 4718596
